TPU v7x, 512 devices: a whole 4x8x8 slice. The times are simulated.
512 devices in a mesh: row: 64 (over z_lo, y, core), vec: 8 (over z_hi, x).
Axes of the slice: x: 4, y: 8, z: 8 (z_hi: 2, z_lo: 4; z = z_hi * 4 + z_lo), core: 2. Of those that a mesh axis runs over, the one named last changes fastest.
Arguments:
- eigvecs: float32 [32768, 8192], P('row', 'vec'), may hold values from -6 to 6
- reflectors: float32 [6, 32768, 128], P(None, 'row', 'vec'), may hold values from -0.375 to 0.375
- factors: float32 [6, 128, 128, 128], P(None, 'row', 'vec'), may hold values from -0.25 to 0.25
Outputs:
- vectors: float32 [32768, 8192], P('row', 'vec')
All inputs are finite; a program needn't handle non-finite values.
Results may differ from a plain program's by a relative error of at most 0.0001.
Values sent between devices are 32-bit elements; how exact they have to be, the bound alone decides.
No kernel may reach another device: no remote copies, remote signals or barrier semaphores. Data moves between devices by JAX's collectives and lax.ppermute only.
A program may use at most 64 MiB of HBM per device.

v0:
```python
import jax
import jax.numpy as jnp
from jax import lax
from jax.sharding import PartitionSpec as P

NB = 128
ROUNDS = 6
highest = lax.Precision.HIGHEST


def gather_turned(arrays, axis, dims):
    turned = [jnp.moveaxis(a, dim, 0) for a, dim in zip(arrays, dims)]
    widths = [t[0].size for t in turned]
    both = jnp.concatenate([t.reshape(-1, w) for t, w in zip(turned, widths)], axis=1)
    whole = lax.all_gather(both, axis, axis=0, tiled=True)
    blocks = jnp.split(whole, [sum(widths[:k]) for k in range(1, len(widths))], axis=1)
    return tuple(
        (
            jnp.moveaxis(b.reshape(-1, *t.shape[1:]), 0, dim)
            for b, t, dim in zip(blocks, turned, dims)
        )
    )


def passed_along(value, axis, steps):
    count = lax.axis_size(axis)
    initial, last = (max(0, -steps), min(count, count - steps))
    return lax.ppermute(value, axis, [(source, source + steps) for source in range(initial, last)])


def product(left, right):
    return jnp.dot(left, right, precision=highest, preferred_element_type=jnp.float32)


def apply_groups(panel, basis, blocks):
    inner = jnp.einsum("gri,grc->gic", basis, panel, precision=highest)
    images = jnp.einsum("gij,gjc->gic", blocks, inner, precision=highest)
    return panel - jnp.einsum("gri,gic->grc", basis, images, precision=highest)


def per_device(eigvecs, reflectors, factors):
    height = eigvecs.shape[0]
    width = eigvecs.shape[1]
    groups = height // (2 * NB)
    reach = (ROUNDS - 1) // 2
    basis_all, blocks_all = gather_turned((reflectors, factors), "vec", (2, 2))
    earlier = passed_along(blocks_all, "row", 1)
    slid = earlier[2:, groups - reach :]
    vectors = eigvecs
    for number in range(ROUNDS):
        behind = number // 2
        if behind > 0:
            blocks = jnp.concatenate(
                [slid[number - 2, reach - behind :], blocks_all[number, : groups - behind]], 0
            )
        else:
            blocks = blocks_all[number]
        basis = basis_all[number]
        if number % 2 == 0:
            panel = apply_groups(
                vectors.reshape(groups, 2 * NB, width), basis.reshape(groups, 2 * NB, NB), blocks
            )
            vectors = panel.reshape(height, width)
        else:
            head_rows = vectors[:NB]
            head_basis = basis[:NB]
            tail_rows = vectors[height - NB :]
            tail_basis = basis[height - NB :]
            last_block = blocks[groups - 1]
            head_inner = product(head_basis.T, head_rows)
            below = passed_along(head_inner, "row", -1)
            tail_inner = product(tail_basis.T, tail_rows) + below
            tail_image = product(last_block, tail_inner)
            above = passed_along(tail_image, "row", 1)
            head_new = head_rows - product(head_basis, above)
            tail_new = tail_rows - product(tail_basis, tail_image)
            middle = apply_groups(
                vectors[NB : height - NB].reshape(groups - 1, 2 * NB, width),
                basis[NB : height - NB].reshape(groups - 1, 2 * NB, NB),
                blocks[: groups - 1],
            ).reshape(height - 2 * NB, width)
            vectors = jnp.concatenate([head_new, middle, tail_new], 0)
    return vectors


def solution(mesh):
    return jax.shard_map(
        per_device,
        mesh=mesh,
        in_specs=(P("row", "vec"), P(None, "row", "vec"), P(None, "row", "vec", None)),
        out_specs=P("row", "vec"),
        check_vma=False,
    )
```

profile of v0, /device:TPU:64, one launch (start us, length us, event | category | flops | bytes accessed | tf_op | source)
XLA Modules:
  0.0 202.4 jit_solution(14676674547720633686)
XLA Ops:
  9.3 88.4 %all-gather.2.cloned.1.call-done = f32[128,4608]{1,0:T(8,128)} async-done(((f32[16,4608]{1,0:T(8,128)}), f32[128,4608]{1,0:T(8,128)}) %all-gather.2.cloned.1.call-update) | async-done | bytes 2359312 | tf_op jit(solution)/shard_map/all_gather | solution.py:15
  97.6 1.4 slice-done
  99.5 1.1 slice-done.1
  101.3 1.9 collective-permute-start.2
  103.2 3.1 %fusion.29 = f32[2,128,1024]{2,1,0:T(8,128)S(1)} fusion(f32[2,256,128]{2,1,0:T(8,128)S(1)} %bitcast.160, f32[2,256,1024]{2,1,0:T(8,128)} %bitcast.153), kind=kOutput, calls=%fused_computation.67 | convolution fusion | flops 805306368 | bytes 3407872 | tf_op jit(solution)/shard_map/gri,grc->gic/dot_general | solution.py:36
  107.3 1.8 convolution_subtract_fusion.2
  110.5 5.8 %collective-permute-start = (f32[128,1024]{1,0:T(8,128)S(1)}, f32[128,1024]{1,0:T(8,128)S(1)}, u32[]{:S(2)}, u32[]{:S(2)}) collective-permute-start(f32[128,1024]{1,0:T(8,128)S(1)} %fusion.13), channel_id=1, source_target_pairs={{8,0},{16,8},{24,16},{32,24},{40,32},{48,40},{56,48},{64,56},{72,6... | collective-permute-start | bytes 1572872 | tf_op jit(solution)/shard_map/ppermute | solution.py:28
  117.8 5.1 %collective-permute-done = f32[128,1024]{1,0:T(8,128)S(1)} collective-permute-done((f32[128,1024]{1,0:T(8,128)S(1)}, f32[128,1024]{1,0:T(8,128)S(1)}, u32[]{:S(2)}, u32[]{:S(2)}) %collective-permute-start) | collective-permute-done | bytes 524320 | tf_op jit(solution)/shard_map/ppermute | solution.py:28
  124.1 2.1 %collective-permute-start.1 = (f32[128,1024]{1,0:T(8,128)S(1)}, f32[128,1024]{1,0:T(8,128)S(1)}, u32[]{:S(2)}, u32[]{:S(2)}) collective-permute-start(f32[128,1024]{1,0:T(8,128)S(1)} %fusion.26), channel_id=1, source_target_pairs={{0,8},{8,16},{16,24},{24,32},{32,40},{40,48},{48,56},{56,64},{64,7... | collective-permute-start | bytes 1572872 | tf_op jit(solution)/shard_map/ppermute | solution.py:28
  126.9 10.0 %collective-permute-done.1 = f32[128,1024]{1,0:T(8,128)S(1)} collective-permute-done((f32[128,1024]{1,0:T(8,128)S(1)}, f32[128,1024]{1,0:T(8,128)S(1)}, u32[]{:S(2)}, u32[]{:S(2)}) %collective-permute-start.1) | collective-permute-done | bytes 524320 | tf_op jit(solution)/shard_map/ppermute | solution.py:28
  137.7 1.3 fusion.30
  140.1 1.9 convolution_subtract_fusion.1
  142.6 1.9 collective-permute-start.3
  145.8 5.4 %collective-permute-done.3 = f32[128,1024]{1,0:T(8,128)S(1)} collective-permute-done((f32[128,1024]{1,0:T(8,128)S(1)}, f32[128,1024]{1,0:T(8,128)S(1)}, u32[]{:S(2)}, u32[]{:S(2)}) %collective-permute-start.3) | collective-permute-done | bytes 524320 | tf_op jit(solution)/shard_map/ppermute | solution.py:28
  152.4 2.1 %collective-permute-start.4 = (f32[128,1024]{1,0:T(8,128)S(1)}, f32[128,1024]{1,0:T(8,128)S(1)}, u32[]{:S(2)}, u32[]{:S(2)}) collective-permute-start(f32[128,1024]{1,0:T(8,128)S(1)} %fusion.24), channel_id=1, source_target_pairs={{0,8},{8,16},{16,24},{24,32},{32,40},{40,48},{48,56},{56,64},{64,7... | collective-permute-start | bytes 1572872 | tf_op jit(solution)/shard_map/ppermute | solution.py:28
  154.6 1.0 convolution_subtract_fusion.4
  156.2 9.0 %collective-permute-done.4 = f32[128,1024]{1,0:T(8,128)S(1)} collective-permute-done((f32[128,1024]{1,0:T(8,128)S(1)}, f32[128,1024]{1,0:T(8,128)S(1)}, u32[]{:S(2)}, u32[]{:S(2)}) %collective-permute-start.4) | collective-permute-done | bytes 524320 | tf_op jit(solution)/shard_map/ppermute | solution.py:28
  166.1 1.3 fusion.31
  168.4 1.9 convolution_subtract_fusion
  170.9 1.9 collective-permute-start.5
  174.2 5.4 %collective-permute-done.5 = f32[128,1024]{1,0:T(8,128)S(1)} collective-permute-done((f32[128,1024]{1,0:T(8,128)S(1)}, f32[128,1024]{1,0:T(8,128)S(1)}, u32[]{:S(2)}, u32[]{:S(2)}) %collective-permute-start.5) | collective-permute-done | bytes 524320 | tf_op jit(solution)/shard_map/ppermute | solution.py:28
  180.7 1.9 collective-permute-start.6
  184.3 9.2 %collective-permute-done.6 = f32[128,1024]{1,0:T(8,128)S(1)} collective-permute-done((f32[128,1024]{1,0:T(8,128)S(1)}, f32[128,1024]{1,0:T(8,128)S(1)}, u32[]{:S(2)}, u32[]{:S(2)}) %collective-permute-start.6) | collective-permute-done | bytes 524320 | tf_op jit(solution)/shard_map/ppermute | solution.py:28
  194.1 1.5 pad_maximum_fusion.2
  (45 shorter events, 22.2 us)
Async XLA Ops:
  6.5 91.1 %all-gather.2.cloned.1.call-start = ((), (), s32[]{:S(2)}) async-start(), calls=%async_computation | async-start | bytes 2654208 | tf_op jit(solution)/shard_map/all_gather | solution.py:15
  97.6 1.4 slice-start
  99.5 1.1 slice-start.1
  101.3 25.6 %collective-permute-start.2 = (f32[6,2,128,128]{3,2,1,0:T(8,128)S(1)}, f32[6,2,128,128]{3,2,1,0:T(8,128)S(1)}, u32[]{:S(2)}, u32[]{:S(2)}) collective-permute-start(f32[6,2,128,128]{3,2,1,0:T(8,128)S(1)} %bitcast.162), channel_id=1, source_target_pairs={{0,8},{8,16},{16,24},{24,32},{32,40},{40,48},{48,56},{56,64},{64,7... | collective-permute-start | bytes 2359304 | tf_op jit(solution)/shard_map/ppermute | solution.py:28
  103.2 4.1 %copy-start = (f32[512,1024]{1,0:T(8,128)S(1)}, f32[512,1024]{1,0:T(8,128)}, u32[]{:S(2)}) copy-start(f32[512,1024]{1,0:T(8,128)} %param.3) | copy-start | bytes 6291460
  110.5 12.4 %collective-permute-start = (f32[128,1024]{1,0:T(8,128)S(1)}, f32[128,1024]{1,0:T(8,128)S(1)}, u32[]{:S(2)}, u32[]{:S(2)}) collective-permute-start(f32[128,1024]{1,0:T(8,128)S(1)} %fusion.13), channel_id=1, source_target_pairs={{8,0},{16,8},{24,16},{32,24},{40,32},{48,40},{56,48},{64,56},{72,6... | collective-permute-start | bytes 1572872 | tf_op jit(solution)/shard_map/ppermute | solution.py:28
  124.1 12.8 %collective-permute-start.1 = (f32[128,1024]{1,0:T(8,128)S(1)}, f32[128,1024]{1,0:T(8,128)S(1)}, u32[]{:S(2)}, u32[]{:S(2)}) collective-permute-start(f32[128,1024]{1,0:T(8,128)S(1)} %fusion.26), channel_id=1, source_target_pairs={{0,8},{8,16},{16,24},{24,32},{32,40},{40,48},{48,56},{56,64},{64,7... | collective-permute-start | bytes 1572872 | tf_op jit(solution)/shard_map/ppermute | solution.py:28
  142.6 8.6 %collective-permute-start.3 = (f32[128,1024]{1,0:T(8,128)S(1)}, f32[128,1024]{1,0:T(8,128)S(1)}, u32[]{:S(2)}, u32[]{:S(2)}) collective-permute-start(f32[128,1024]{1,0:T(8,128)S(1)} %fusion.10), channel_id=1, source_target_pairs={{8,0},{16,8},{24,16},{32,24},{40,32},{48,40},{56,48},{64,56},{72,6... | collective-permute-start | bytes 1572872 | tf_op jit(solution)/shard_map/ppermute | solution.py:28
  152.4 12.8 %collective-permute-start.4 = (f32[128,1024]{1,0:T(8,128)S(1)}, f32[128,1024]{1,0:T(8,128)S(1)}, u32[]{:S(2)}, u32[]{:S(2)}) collective-permute-start(f32[128,1024]{1,0:T(8,128)S(1)} %fusion.24), channel_id=1, source_target_pairs={{0,8},{8,16},{16,24},{24,32},{32,40},{40,48},{48,56},{56,64},{64,7... | collective-permute-start | bytes 1572872 | tf_op jit(solution)/shard_map/ppermute | solution.py:28
  170.9 8.6 %collective-permute-start.5 = (f32[128,1024]{1,0:T(8,128)S(1)}, f32[128,1024]{1,0:T(8,128)S(1)}, u32[]{:S(2)}, u32[]{:S(2)}) collective-permute-start(f32[128,1024]{1,0:T(8,128)S(1)} %fusion.7), channel_id=1, source_target_pairs={{8,0},{16,8},{24,16},{32,24},{40,32},{48,40},{56,48},{64,56},{72,6... | collective-permute-start | bytes 1572872 | tf_op jit(solution)/shard_map/ppermute | solution.py:28
  180.7 12.8 %collective-permute-start.6 = (f32[128,1024]{1,0:T(8,128)S(1)}, f32[128,1024]{1,0:T(8,128)S(1)}, u32[]{:S(2)}, u32[]{:S(2)}) collective-permute-start(f32[128,1024]{1,0:T(8,128)S(1)} %fusion.22), channel_id=1, source_target_pairs={{0,8},{8,16},{16,24},{24,32},{32,40},{40,48},{48,56},{56,64},{64,7... | collective-permute-start | bytes 1572872 | tf_op jit(solution)/shard_map/ppermute | solution.py:28
Sparse Core Ops, SparseCore 0:
  10.5 87.0 all-gather.1
where the time goes:
time: 203 us; the launch traced here: 202 us
  waiting for transfers between devices  132 us (65%)
  matrix products  30.2 us (15%)
  starting transfers between devices  17.7 us (9%)
  between operations  13.8 us (7%)
  local copies, waits for them, and re-layouts  5.56 us (3%)
  other arithmetic  2.67 us (1%)
    all_gather x1, waiting for transfers between devices, gather_turned(): whole = lax.all_gather(both, axis, axis=0, tiled=True)  88.4 us
    ppermute x7, waiting for transfers between devices, passed_along(): lax.ppermute(value, axis, [(source, source + steps) for source in range(i...  44.1 us
    ppermute x7, starting transfers between devices, passed_along(): lax.ppermute(value, axis, [(source, source + steps) for source in range(i...  17.7 us
    dot_general x15, matrix products, product(): jnp.dot(left, right, precision=highest, preferred_element_type=jnp.float32)  9.06 us
    dot_general x6, matrix products, apply_groups(): return panel - jnp.einsum('gri,gic->grc', basis, images, precision=highest)  8.62 us
    dot_general x6, matrix products, apply_groups(): inner = jnp.einsum('gri,grc->gic', basis, panel, precision=highest)  7.84 us
    dot_general x6, matrix products, apply_groups(): images = jnp.einsum('gij,gjc->gic', blocks, inner, precision=highest)  4.71 us
  transfers between devices with their start and end apart: 8, of which 7 were waited for; matrix products, arithmetic and copies ran while one was open for 8% of the time, Pallas kernels for 0%

commit v1 on v0

--- a/solution.py
+++ b/solution.py
@@ -12,7 +12,9 @@
     turned = [jnp.moveaxis(a, dim, 0) for a, dim in zip(arrays, dims)]
     widths = [t[0].size for t in turned]
     both = jnp.concatenate([t.reshape(-1, w) for t, w in zip(turned, widths)], axis=1)
-    whole = lax.all_gather(both, axis, axis=0, tiled=True)
+    whole = jnp.concatenate(
+        lax.all_to_all(jnp.stack([both] * lax.axis_size(axis)), axis, 0, 0), axis=0
+    )
     blocks = jnp.split(whole, [sum(widths[:k]) for k in range(1, len(widths))], axis=1)
     return tuple(
         (

time: 203 us -> 171 us (0.84)
  waiting for transfers between devices: 132 us -> 44.1 us
  blocking collectives: 0 us -> 70.5 us
  between operations: 13.8 us -> 0.44 us
    all_gather x1 -> x0, waiting for transfers between devices: 88.4 us -> none  [gather_turned(): whole = lax.all_gather(both, axis, axis=0, tiled=True)]
    all_to_all x0 -> x1, blocking collectives: none -> 70.5 us  [gather_turned(): lax.all_to_all(jnp.stack([both] * lax.axis_size(axis)), axis, 0, 0)]
  transfers between devices with their start and end apart: 8 -> 7, of which waited for: 7 -> 6; matrix products, arithmetic and copies ran while one was open for 8% -> 10% of each run, Pallas kernels for 0% -> 0%
where the time goes in v1:
time: 171 us; the launch traced here: 170 us
  blocking collectives  70.5 us (41%)
  waiting for transfers between devices  44.1 us (26%)
  matrix products  30.2 us (18%)
  starting transfers between devices  17.7 us (10%)
  local copies, waits for them, and re-layouts  5.42 us (3%)
  other arithmetic  1.95 us (1%)
    all_to_all x1, blocking collectives, gather_turned(): lax.all_to_all(jnp.stack([both] * lax.axis_size(axis)), axis, 0, 0)  70.5 us
    ppermute x7, waiting for transfers between devices, passed_along(): lax.ppermute(value, axis, [(source, source + steps) for source in range(i...  44.1 us
    ppermute x7, starting transfers between devices, passed_along(): lax.ppermute(value, axis, [(source, source + steps) for source in range(i...  17.7 us
    dot_general x15, matrix products, product(): jnp.dot(left, right, precision=highest, preferred_element_type=jnp.float32)  9.06 us
    dot_general x6, matrix products, apply_groups(): return panel - jnp.einsum('gri,gic->grc', basis, images, precision=highest)  8.62 us
    dot_general x6, matrix products, apply_groups(): inner = jnp.einsum('gri,grc->gic', basis, panel, precision=highest)  7.84 us
    dot_general x6, matrix products, apply_groups(): images = jnp.einsum('gij,gjc->gic', blocks, inner, precision=highest)  4.71 us
  transfers between devices with their start and end apart: 7, of which 6 were waited for; matrix products, arithmetic and copies ran while one was open for 10% of the time, Pallas kernels for 0%

profile of v1, /device:TPU:64, one launch (start us, length us, event | category | flops | bytes accessed | tf_op | source)
XLA Modules:
  0.0 170.4 jit_solution(7680173677217426416)
XLA Ops:
  2.2 70.5 %all_to_all.5 = f32[8,16,4608]{2,1,0:T(8,128)S(1)} all-to-all(f32[8,16,4608]{2,1,0:T(8,128)S(1)} %stack.2), channel_id=1, replica_groups=mesh['row'=64,'vec'=8] {'vec'}, dimensions={0} | all-to-all | bytes 4718592 | tf_op jit(solution)/shard_map/all_to_all | solution.py:16
  74.3 1.4 copy.17
  76.0 1.9 %collective-permute-start.2 = (f32[6,2,128,128]{3,2,1,0:T(8,128)S(1)}, f32[6,2,128,128]{3,2,1,0:T(8,128)S(1)}, u32[]{:S(2)}, u32[]{:S(2)}) collective-permute-start(f32[6,2,128,128]{3,2,1,0:T(8,128)S(1)} %bitcast.165), channel_id=1, source_target_pairs={{0,8},{8,16},{16,24},{24,32},{32,40},{40,48},{48,56},{56,64},{64,7... | collective-permute-start | bytes 2359304 | tf_op jit(solution)/shard_map/ppermute | solution.py:30
  78.0 3.1 %fusion.29 = f32[2,128,1024]{2,1,0:T(8,128)S(1)} fusion(f32[2,256,128]{2,1,0:T(8,128)S(1)} %bitcast.163, f32[2,256,1024]{2,1,0:T(8,128)} %bitcast.156), kind=kOutput, calls=%fused_computation.67 | convolution fusion | flops 805306368 | bytes 3407872 | tf_op jit(solution)/shard_map/gri,grc->gic/dot_general | solution.py:38
  82.0 1.8 %convolution_subtract_fusion.2 = f32[2,256,1024]{2,1,0:T(8,128)S(1)} fusion(f32[2,256,1024]{2,1,0:T(8,128)S(1)} %bitcast.157, f32[2,256,128]{2,1,0:T(8,128)S(1)} %bitcast.164, f32[2,128,1024]{2,1,0:T(8,128)S(1)} %fusion.16), kind=kOutput, calls=%fused_computation.5 | convolution fusion | flops 805830656 | bytes 5505024 | tf_op jit(solution)/shard_map/gri,gic->grc/dot_general | solution.py:40
  85.2 5.7 %collective-permute-start = (f32[128,1024]{1,0:T(8,128)S(1)}, f32[128,1024]{1,0:T(8,128)S(1)}, u32[]{:S(2)}, u32[]{:S(2)}) collective-permute-start(f32[128,1024]{1,0:T(8,128)S(1)} %fusion.13), channel_id=1, source_target_pairs={{8,0},{16,8},{24,16},{32,24},{40,32},{48,40},{56,48},{64,56},{72,6... | collective-permute-start | bytes 1572872 | tf_op jit(solution)/shard_map/ppermute | solution.py:30
  92.6 5.1 %collective-permute-done = f32[128,1024]{1,0:T(8,128)S(1)} collective-permute-done((f32[128,1024]{1,0:T(8,128)S(1)}, f32[128,1024]{1,0:T(8,128)S(1)}, u32[]{:S(2)}, u32[]{:S(2)}) %collective-permute-start) | collective-permute-done | bytes 524320 | tf_op jit(solution)/shard_map/ppermute | solution.py:30
  98.9 2.1 %collective-permute-start.1 = (f32[128,1024]{1,0:T(8,128)S(1)}, f32[128,1024]{1,0:T(8,128)S(1)}, u32[]{:S(2)}, u32[]{:S(2)}) collective-permute-start(f32[128,1024]{1,0:T(8,128)S(1)} %fusion.26), channel_id=1, source_target_pairs={{0,8},{8,16},{16,24},{24,32},{32,40},{40,48},{48,56},{56,64},{64,7... | collective-permute-start | bytes 1572872 | tf_op jit(solution)/shard_map/ppermute | solution.py:30
  101.6 10.0 %collective-permute-done.1 = f32[128,1024]{1,0:T(8,128)S(1)} collective-permute-done((f32[128,1024]{1,0:T(8,128)S(1)}, f32[128,1024]{1,0:T(8,128)S(1)}, u32[]{:S(2)}, u32[]{:S(2)}) %collective-permute-start.1) | collective-permute-done | bytes 524320 | tf_op jit(solution)/shard_map/ppermute | solution.py:30
  112.5 1.3 fusion.30
  114.8 1.9 %convolution_subtract_fusion.1 = f32[2,256,1024]{2,1,0:T(8,128)S(1)} fusion(f32[2,256,1024]{2,1,0:T(8,128)S(1)} %bitcast.132, f32[2,256,128]{2,1,0:T(8,128)S(1)} %bitcast.162, f32[2,128,1024]{2,1,0:T(8,128)S(1)} %fusion.17), kind=kOutput, calls=%fused_computation.4 | convolution fusion | flops 805830656 | bytes 5505024 | tf_op jit(solution)/shard_map/gri,gic->grc/dot_general | solution.py:40
  117.4 1.9 %collective-permute-start.3 = (f32[128,1024]{1,0:T(8,128)S(1)}, f32[128,1024]{1,0:T(8,128)S(1)}, u32[]{:S(2)}, u32[]{:S(2)}) collective-permute-start(f32[128,1024]{1,0:T(8,128)S(1)} %fusion.10), channel_id=1, source_target_pairs={{8,0},{16,8},{24,16},{32,24},{40,32},{48,40},{56,48},{64,56},{72,6... | collective-permute-start | bytes 1572872 | tf_op jit(solution)/shard_map/ppermute | solution.py:30
  120.6 5.4 %collective-permute-done.3 = f32[128,1024]{1,0:T(8,128)S(1)} collective-permute-done((f32[128,1024]{1,0:T(8,128)S(1)}, f32[128,1024]{1,0:T(8,128)S(1)}, u32[]{:S(2)}, u32[]{:S(2)}) %collective-permute-start.3) | collective-permute-done | bytes 524320 | tf_op jit(solution)/shard_map/ppermute | solution.py:30
  127.2 2.1 %collective-permute-start.4 = (f32[128,1024]{1,0:T(8,128)S(1)}, f32[128,1024]{1,0:T(8,128)S(1)}, u32[]{:S(2)}, u32[]{:S(2)}) collective-permute-start(f32[128,1024]{1,0:T(8,128)S(1)} %fusion.24), channel_id=1, source_target_pairs={{0,8},{8,16},{16,24},{24,32},{32,40},{40,48},{48,56},{56,64},{64,7... | collective-permute-start | bytes 1572872 | tf_op jit(solution)/shard_map/ppermute | solution.py:30
  129.4 1.0 convolution_subtract_fusion.4
  131.0 9.0 %collective-permute-done.4 = f32[128,1024]{1,0:T(8,128)S(1)} collective-permute-done((f32[128,1024]{1,0:T(8,128)S(1)}, f32[128,1024]{1,0:T(8,128)S(1)}, u32[]{:S(2)}, u32[]{:S(2)}) %collective-permute-start.4) | collective-permute-done | bytes 524320 | tf_op jit(solution)/shard_map/ppermute | solution.py:30
  140.8 1.3 fusion.31
  143.1 1.9 %convolution_subtract_fusion = f32[2,256,1024]{2,1,0:T(8,128)S(1)} fusion(f32[2,256,1024]{2,1,0:T(8,128)S(1)} %bitcast.134, f32[2,256,128]{2,1,0:T(8,128)S(1)} %bitcast.160, f32[2,128,1024]{2,1,0:T(8,128)S(1)} %fusion.15), kind=kOutput, calls=%fused_computation.3 | convolution fusion | flops 805830656 | bytes 5505024 | tf_op jit(solution)/shard_map/gri,gic->grc/dot_general | solution.py:40
  145.7 1.9 %collective-permute-start.5 = (f32[128,1024]{1,0:T(8,128)S(1)}, f32[128,1024]{1,0:T(8,128)S(1)}, u32[]{:S(2)}, u32[]{:S(2)}) collective-permute-start(f32[128,1024]{1,0:T(8,128)S(1)} %fusion.7), channel_id=1, source_target_pairs={{8,0},{16,8},{24,16},{32,24},{40,32},{48,40},{56,48},{64,56},{72,6... | collective-permute-start | bytes 1572872 | tf_op jit(solution)/shard_map/ppermute | solution.py:30
  148.9 5.4 %collective-permute-done.5 = f32[128,1024]{1,0:T(8,128)S(1)} collective-permute-done((f32[128,1024]{1,0:T(8,128)S(1)}, f32[128,1024]{1,0:T(8,128)S(1)}, u32[]{:S(2)}, u32[]{:S(2)}) %collective-permute-start.5) | collective-permute-done | bytes 524320 | tf_op jit(solution)/shard_map/ppermute | solution.py:30
  155.5 1.9 %collective-permute-start.6 = (f32[128,1024]{1,0:T(8,128)S(1)}, f32[128,1024]{1,0:T(8,128)S(1)}, u32[]{:S(2)}, u32[]{:S(2)}) collective-permute-start(f32[128,1024]{1,0:T(8,128)S(1)} %fusion.22), channel_id=1, source_target_pairs={{0,8},{8,16},{16,24},{24,32},{32,40},{40,48},{48,56},{56,64},{64,7... | collective-permute-start | bytes 1572872 | tf_op jit(solution)/shard_map/ppermute | solution.py:30
  157.4 1.0 convolution_subtract_fusion.3
  159.1 9.2 %collective-permute-done.6 = f32[128,1024]{1,0:T(8,128)S(1)} collective-permute-done((f32[128,1024]{1,0:T(8,128)S(1)}, f32[128,1024]{1,0:T(8,128)S(1)}, u32[]{:S(2)}, u32[]{:S(2)}) %collective-permute-start.6) | collective-permute-done | bytes 524320 | tf_op jit(solution)/shard_map/ppermute | solution.py:30
  168.9 1.5 pad_maximum_fusion.2
  (42 shorter events, 21.4 us)
Async XLA Ops:
  76.0 25.6 %collective-permute-start.2 = (f32[6,2,128,128]{3,2,1,0:T(8,128)S(1)}, f32[6,2,128,128]{3,2,1,0:T(8,128)S(1)}, u32[]{:S(2)}, u32[]{:S(2)}) collective-permute-start(f32[6,2,128,128]{3,2,1,0:T(8,128)S(1)} %bitcast.165), channel_id=1, source_target_pairs={{0,8},{8,16},{16,24},{24,32},{32,40},{40,48},{48,56},{56,64},{64,7... | collective-permute-start | bytes 2359304 | tf_op jit(solution)/shard_map/ppermute | solution.py:30
  78.0 4.1 %copy-start = (f32[512,1024]{1,0:T(8,128)S(1)}, f32[512,1024]{1,0:T(8,128)}, u32[]{:S(2)}) copy-start(f32[512,1024]{1,0:T(8,128)} %param.3) | copy-start | bytes 6291460
  85.2 12.4 %collective-permute-start = (f32[128,1024]{1,0:T(8,128)S(1)}, f32[128,1024]{1,0:T(8,128)S(1)}, u32[]{:S(2)}, u32[]{:S(2)}) collective-permute-start(f32[128,1024]{1,0:T(8,128)S(1)} %fusion.13), channel_id=1, source_target_pairs={{8,0},{16,8},{24,16},{32,24},{40,32},{48,40},{56,48},{64,56},{72,6... | collective-permute-start | bytes 1572872 | tf_op jit(solution)/shard_map/ppermute | solution.py:30
  98.9 12.8 %collective-permute-start.1 = (f32[128,1024]{1,0:T(8,128)S(1)}, f32[128,1024]{1,0:T(8,128)S(1)}, u32[]{:S(2)}, u32[]{:S(2)}) collective-permute-start(f32[128,1024]{1,0:T(8,128)S(1)} %fusion.26), channel_id=1, source_target_pairs={{0,8},{8,16},{16,24},{24,32},{32,40},{40,48},{48,56},{56,64},{64,7... | collective-permute-start | bytes 1572872 | tf_op jit(solution)/shard_map/ppermute | solution.py:30
  117.4 8.6 %collective-permute-start.3 = (f32[128,1024]{1,0:T(8,128)S(1)}, f32[128,1024]{1,0:T(8,128)S(1)}, u32[]{:S(2)}, u32[]{:S(2)}) collective-permute-start(f32[128,1024]{1,0:T(8,128)S(1)} %fusion.10), channel_id=1, source_target_pairs={{8,0},{16,8},{24,16},{32,24},{40,32},{48,40},{56,48},{64,56},{72,6... | collective-permute-start | bytes 1572872 | tf_op jit(solution)/shard_map/ppermute | solution.py:30
  127.2 12.8 %collective-permute-start.4 = (f32[128,1024]{1,0:T(8,128)S(1)}, f32[128,1024]{1,0:T(8,128)S(1)}, u32[]{:S(2)}, u32[]{:S(2)}) collective-permute-start(f32[128,1024]{1,0:T(8,128)S(1)} %fusion.24), channel_id=1, source_target_pairs={{0,8},{8,16},{16,24},{24,32},{32,40},{40,48},{48,56},{56,64},{64,7... | collective-permute-start | bytes 1572872 | tf_op jit(solution)/shard_map/ppermute | solution.py:30
  145.7 8.6 %collective-permute-start.5 = (f32[128,1024]{1,0:T(8,128)S(1)}, f32[128,1024]{1,0:T(8,128)S(1)}, u32[]{:S(2)}, u32[]{:S(2)}) collective-permute-start(f32[128,1024]{1,0:T(8,128)S(1)} %fusion.7), channel_id=1, source_target_pairs={{8,0},{16,8},{24,16},{32,24},{40,32},{48,40},{56,48},{64,56},{72,6... | collective-permute-start | bytes 1572872 | tf_op jit(solution)/shard_map/ppermute | solution.py:30
  155.5 12.8 %collective-permute-start.6 = (f32[128,1024]{1,0:T(8,128)S(1)}, f32[128,1024]{1,0:T(8,128)S(1)}, u32[]{:S(2)}, u32[]{:S(2)}) collective-permute-start(f32[128,1024]{1,0:T(8,128)S(1)} %fusion.22), channel_id=1, source_target_pairs={{0,8},{8,16},{16,24},{24,32},{32,40},{40,48},{48,56},{56,64},{64,7... | collective-permute-start | bytes 1572872 | tf_op jit(solution)/shard_map/ppermute | solution.py:30
